TPU v7x, 256 devices: a whole 4x4x8 slice. The times are simulated.
256 devices in a mesh: frames: 64 (over y_hi, z, x), rows: 4 (over y_lo, core).
Axes of the slice: x: 4, y: 4 (y_hi: 2, y_lo: 2; y = y_hi * 2 + y_lo), z: 8, core: 2. Of those that a mesh axis runs over, the one named last changes fastest.
Arguments:
- video: bfloat16 [64, 32, 160, 512], P('frames', 'rows'), may hold values from -6 to 6
- norm1_gain: float32 [512], replicated, may hold values from 0.25 to 1.75
- norm1_shift: float32 [512], replicated, may hold values from -1.75 to 1.75
- conv1_weight: bfloat16 [3, 3, 512, 512], replicated, may hold values from -0.09375 to 0.09375
- conv1_bias: float32 [512], replicated, may hold values from -1.75 to 1.75
- norm2_gain: float32 [512], replicated, may hold values from 0.25 to 1.75
- norm2_shift: float32 [512], replicated, may hold values from -1.75 to 1.75
- conv2_weight: bfloat16 [3, 3, 512, 512], replicated, may hold values from -0.09375 to 0.09375
- conv2_bias: float32 [512], replicated, may hold values from -1.75 to 1.75
- out_gain: float32 [512], replicated, may hold values from 0.25 to 1.75
- out_shift: float32 [512], replicated, may hold values from -1.75 to 1.75
- out_weight: bfloat16 [3, 3, 512, 8], replicated, may hold values from -0.09375 to 0.09375
- out_bias: float32 [8], replicated, may hold values from -1.75 to 1.75
- quant_weight: float32 [8, 4], replicated, may hold values from -2 to 2
- quant_bias: float32 [4], replicated, may hold values from -1.75 to 1.75
- time_in_weight: bfloat16 [3, 3, 3, 4, 128], replicated, may hold values from -0.625 to 0.625
- time_in_bias: float32 [128], replicated, may hold values from -1.75 to 1.75
- tnorm1_gain: float32 [128], replicated, may hold values from 0.25 to 1.75
- tnorm1_shift: float32 [128], replicated, may hold values from -1.75 to 1.75
- time1_weight: bfloat16 [3, 3, 3, 128, 128], replicated, may hold values from -0.109375 to 0.109375
- tnorm2_gain: float32 [128], replicated, may hold values from 0.25 to 1.75
- tnorm2_shift: float32 [128], replicated, may hold values from -1.75 to 1.75
- time2_weight: bfloat16 [3, 3, 3, 128, 128], replicated, may hold values from -0.109375 to 0.109375
- time2_bias: float32 [128], replicated, may hold values from -1.75 to 1.75
Outputs:
- features: bfloat16 [64, 32, 160, 128], P('frames', 'rows')
All inputs are finite; a program needn't handle non-finite values.
Results may differ from a plain program's by a relative error of at most 0.01.
Values may be sent and summed in bfloat16 or wider, within the bound.
A program may use at most 64 MiB of HBM per device.

v0:
```python
import functools

import jax
import jax.numpy as jnp
from jax import lax
from jax.experimental import pallas as pl
from jax.experimental.pallas import tpu as pltpu
from jax.sharding import PartitionSpec as P

GROUPS = 32
EPS = 1e-06
LATENT_SCALE = 0.13025

R = 8
W = 160
C = 512
T = 128
LANES = 256
BACK = 6

MESH = pl.DeviceIdType.MESH
F32 = jnp.float32
BF16 = jnp.bfloat16


def lane_group_sum(x, size):
    lane = lax.broadcasted_iota(jnp.int32, x.shape, 1)
    step = 1
    while step < size:
        up = pltpu.roll(x, step, 1)
        down = pltpu.roll(x, 128 - step, 1)
        x = x + jnp.where((lane // step) % 2 == 1, up, down)
        step *= 2
    return x


def column_shifts(a):
    col = lax.broadcasted_iota(jnp.int32, a.shape, 0)
    left = jnp.where(col == 0, 0.0, pltpu.roll(a, 1, 0))
    right = jnp.where(col == W - 1, 0.0, pltpu.roll(a, W - 1, 0))
    return left.astype(BF16), a.astype(BF16), right.astype(BF16)


def half_silu(v, scale, shift):
    w = v * scale + shift
    return w * jnp.tanh(w) + w


def partial_sums(v):
    g = v.reshape(-1, 8, v.shape[-1])
    return jnp.sum(g, axis=0), jnp.sum(g * g, axis=0)


def kernel(
    n_frames,
    n_rows,
    video, g1, s1, cw1, cb1, g2, s2, cw2, cb2, g3, s3, ow, ob, qw, qb,
    tiw, tib, tg1, ts1, tw1, tg2, ts2, tw2, tb2,
    out,
    vid, w1, w2, act, h, hsend, hrecv, ysend, yrecv,
    params, cbias, tparams, obv, qwv, qbv, tiwv,
    wht, pt, mom, wbf, wb, w1r, w2r,
    stbuf, tstbuf, latsend, lx, ltt, t0s, b1, t1s, b2, outv,
    in_sem, vh_sem, hh_sem, yh_sem, st_sem, lat_send, lat_recv,
):
    f = lax.axis_index("frames")
    rr = lax.axis_index("rows")

    def local(src, dst, k):
        return pltpu.make_async_copy(src, dst, in_sem.at[k])

    c_vid = local(video, vid.at[pl.ds(1, R)], 0)
    c_w1 = local(cw1, w1, 1)
    c_w2 = local(cw2, w2, 2)
    c_par = [local(a, params.at[i], 3 + i) for i, a in enumerate((g1, s1, g2, s2, g3, s3))]
    c_cb = [local(a, cbias.at[i], 9 + i) for i, a in enumerate((cb1, cb2))]
    c_tp = [local(a, tparams.at[i], 11 + i) for i, a in enumerate((tib, tg1, ts1, tg2, ts2, tb2))]
    c_ow = local(ow, wht, 17)
    c_q = [local(ob, obv, 18), local(qw, qwv, 19), local(qb, qbv, 20)]
    c_tiw = local(tiw, tiwv, 21)
    c_t = []
    for i, (src, dst) in enumerate(((tw1, w1r), (tw2, w2r))):
        for p in range(2):
            c_t.append(local(src, dst.at[:, pl.ds(p, 3), :, pl.ds(T * p, T)], 22 + 2 * i + p))

    def begin(copies):
        for c in copies:
            c.start()

    def finish(copies):
        for c in copies:
            c.wait()

    def lat_targets():
        for k in range(BACK + 1):
            for d in (-1, 0, 1):
                if k or d:
                    yield k, d

    def sends_to(k, d):
        ok = f + k < n_frames
        if d == -1:
            ok = jnp.logical_and(ok, rr > 0)
        if d == 1:
            ok = jnp.logical_and(ok, rr < n_rows - 1)
        return ok

    def gets_from(k, d):
        ok = f >= k
        if d == -1:
            ok = jnp.logical_and(ok, rr < n_rows - 1)
        if d == 1:
            ok = jnp.logical_and(ok, rr > 0)
        return ok

    c_vid.start()
    barrier = pltpu.get_barrier_semaphore()
    for d in range(1, n_rows):
        pl.semaphore_signal(
            barrier, inc=1, device_id={"frames": f, "rows": lax.rem(rr + d, n_rows)},
            device_id_type=MESH,
        )
    for k, d in lat_targets():
        if k:
            @pl.when(gets_from(k, d))
            def _():
                pl.semaphore_signal(
                    barrier, inc=1, device_id={"frames": f - k, "rows": rr - d}, device_id_type=MESH
                )

    begin(c_par + c_cb + c_tp + [c_ow] + c_q + [c_tiw])

    def halo(src_last, src_first, dst_above, dst_below, sem):
        down = pltpu.make_async_remote_copy(
            src_ref=src_last, dst_ref=dst_above, send_sem=sem.at[0], recv_sem=sem.at[1],
            device_id={"frames": f, "rows": rr + 1}, device_id_type=MESH,
        )
        up = pltpu.make_async_remote_copy(
            src_ref=src_first, dst_ref=dst_below, send_sem=sem.at[2], recv_sem=sem.at[3],
            device_id={"frames": f, "rows": rr - 1}, device_id_type=MESH,
        )
        return down, up

    has_above = rr > 0
    has_below = rr < n_rows - 1

    def stat_copies(buf, e):
        return [
            pltpu.make_async_remote_copy(
                src_ref=buf.at[rr], dst_ref=buf.at[rr],
                send_sem=st_sem.at[e, 0, d - 1], recv_sem=st_sem.at[e, 1, d - 1],
                device_id={"frames": f, "rows": lax.rem(rr + d, n_rows)}, device_id_type=MESH,
            )
            for d in range(1, n_rows)
        ]

    def send_stats(e, s, q):
        s = jnp.sum(s, axis=0, keepdims=True)
        q = jnp.sum(q, axis=0, keepdims=True)
        for t in range(C // 128):
            stbuf[e, rr, t : t + 1, :] = s[:, 128 * t : 128 * t + 128]
            stbuf[e, rr, 4 + t : 5 + t, :] = q[:, 128 * t : 128 * t + 128]
        copies = stat_copies(stbuf.at[e], e)
        begin(copies)
        return copies

    def norm_terms(e, copies, gain, shift):
        finish(copies)
        total = stbuf[e, 0]
        for r in range(1, n_rows):
            total = total + stbuf[e, r]
        total = lane_group_sum(total, C // GROUPS) * (1.0 / (n_rows * R * W * (C // GROUPS)))
        mean = total[0:4]
        var = jnp.maximum(total[4:8] - mean * mean, 0.0)
        scale = lax.rsqrt(var + EPS) * gain
        shift = shift - mean * scale
        wide = lambda x: jnp.concatenate([x[t : t + 1] for t in range(C // 128)], axis=1) * 0.5
        return wide(scale), wide(shift)

    def put_line(line, v, scale, shift, shifted=True):
        a = half_silu(v, scale, shift)
        if shifted:
            for j, x in enumerate(column_shifts(a)):
                act[j, line] = x
        else:
            act[1, line] = a.astype(BF16)

    def halo_lines(copies, above, below, scale, shift, shifted=True):
        taps = range(3) if shifted else (1,)
        for has, copy, ref, line in (
            (has_above, copies[0], above, 0),
            (has_below, copies[1], below, R + 1),
        ):
            @pl.when(has)
            def _():
                copy.wait_recv()
                put_line(line, ref[...].astype(F32), scale, shift, shifted)

            @pl.when(jnp.logical_not(has))
            def _():
                for j in taps:
                    act[j, line] = jnp.zeros((W, C), BF16)

    def start_down(copies):
        @pl.when(has_below)
        def _():
            copies[0].start()

    def start_up(copies):
        @pl.when(has_above)
        def _():
            copies[1].start()

    def end_sends(copies):
        @pl.when(has_below)
        def _():
            copies[0].wait_send()

        @pl.when(has_above)
        def _():
            copies[1].wait_send()

    def conv(weight, finish_line):
        def block(b, carry):
            s, q = carry
            lo = 2 * b
            hi = R - 2 - 2 * b
            acc = None
            for i in range(3):
                for j in range(3):
                    lhs = jnp.concatenate(
                        [
                            act[j, pl.ds(lo + i, 2)].reshape(2 * W, C),
                            act[j, pl.ds(hi + i, 2)].reshape(2 * W, C),
                        ],
                        axis=0,
                    )
                    d = jnp.dot(lhs, weight[3 * i + j], preferred_element_type=F32)
                    acc = d if acc is None else acc + d
            return finish_line(b, lo, hi, acc, s, q)

        zero = jnp.zeros((8, C), F32)
        return lax.fori_loop(0, 2, block, (zero, zero))

    tstbuf[...] = jnp.zeros(tstbuf.shape, F32)
    c_vid.wait()
    c_w1.start()

    def video_sums(r, carry):
        s, q = carry
        a, b = partial_sums(vid[r + 1].astype(F32))
        return s + a, q + b

    zero = jnp.zeros((8, C), F32)
    s, q = lax.fori_loop(0, R, video_sums, (zero, zero))

    later = sum(1 - lax.div(f + k, n_frames) for k in range(1, BACK + 1))
    lines = 2 + lax.div(rr + n_rows - 1, n_rows) - lax.div(rr + 1, n_rows)
    pl.semaphore_wait(barrier, n_rows - 1 + later * lines)

    copies = send_stats(0, s, q)
    vh = halo(vid.at[R], vid.at[1], vid.at[0], vid.at[R + 1], vh_sem)
    start_down(vh)
    start_up(vh)
    c_w2.start()
    begin(c_t)

    finish([c_tiw])
    wbf[...] = jnp.zeros(wbf.shape, F32)
    for t in range(3):
        for j in range(3):
            for i in range(3):
                piece = tiwv[t, i, j].astype(F32)
                for n in range(R + 4):
                    top = 64 * j + 4 * (n + 1 + i)
                    wbf[top : top + 4, T * n : T * n + T] = piece
        for n in range(3):
            wb[n, 256 * t : 256 * t + 256] = wbf[:, 512 * n : 512 * n + 512].astype(BF16)

    finish(c_par + c_cb)
    scale, shift = norm_terms(0, copies, params[0], params[1])

    def video_line(r, _):
        put_line(r + 1, vid[r + 1].astype(F32), scale, shift)
        return 0

    lax.fori_loop(0, R, video_line, 0)
    halo_lines(vh, vid.at[0], vid.at[R + 1], scale, shift)
    c_w1.wait()

    hh = halo(hsend.at[1], hsend.at[0], hrecv.at[0], hrecv.at[1], hh_sem)

    def h_lines(b, lo, hi, acc, s, q):
        v = acc + cbias[0]
        h[pl.ds(lo, 2)] = v[: 2 * W].reshape(2, W, C)
        h[pl.ds(hi, 2)] = v[2 * W :].reshape(2, W, C)

        @pl.when(b == 0)
        def _():
            hsend[0] = v[:W].astype(BF16)
            hsend[1] = v[3 * W :].astype(BF16)
            start_down(hh)
            start_up(hh)

        a, c = partial_sums(v)
        return s + a, q + c

    s, q = conv(w1, h_lines)
    copies = send_stats(1, s, q)

    finish([c_ow] + c_q + c_tp)
    nt = (((1,), (1,)), ((), ()))
    pt[...] = jnp.zeros(pt.shape, F32)
    for t in range(3):
        for dst in (w1r, w2r):
            dst[t, 3, :, 0:T] = jnp.zeros((3 * T, T), BF16)
            dst[t, 0, :, T : 2 * T] = jnp.zeros((3 * T, T), BF16)
    row = lax.broadcasted_iota(jnp.int32, (4 * R, 8 * R), 0)
    col = lax.broadcasted_iota(jnp.int32, (4 * R, 8 * R), 1)
    quant = jnp.zeros((4 * R, 8 * R), F32)
    for m in range(8):
        for c in range(4):
            hit = (row % 4 == c) & (col % 8 == m) & (row // 4 == col // 8)
            quant = quant + jnp.where(hit, qwv[c : c + 1, m : m + 1], 0.0)
    row8 = lax.broadcasted_iota(jnp.int32, (8 * R, 1), 0)
    row4 = lax.broadcasted_iota(jnp.int32, (4 * R, 1), 0)
    head_bias = jnp.zeros((8 * R, 1), F32)
    for m in range(8):
        head_bias = head_bias + jnp.where(row8 % 8 == m, obv[0:1, m : m + 1], 0.0)
    quant_bias = jnp.zeros((4 * R, 1), F32)
    for c in range(4):
        quant_bias = quant_bias + jnp.where(row4 % 4 == c, qbv[0:1, c : c + 1], 0.0)

    scale, shift = norm_terms(1, copies, params[2], params[3])

    def h_line(r, _):
        put_line(r + 1, h[r], scale, shift)
        return 0

    lax.fori_loop(0, R, h_line, 0)
    halo_lines(hh, hrecv.at[0], hrecv.at[1], scale, shift)
    c_w2.wait()

    yh = halo(ysend.at[1], ysend.at[0], yrecv.at[0], yrecv.at[1], yh_sem)

    def y_lines(b, lo, hi, acc, s, q):
        res = jnp.concatenate(
            [vid[pl.ds(lo + 1, 2)].reshape(2 * W, C), vid[pl.ds(hi + 1, 2)].reshape(2 * W, C)],
            axis=0,
        )
        v = res.astype(F32) + (acc + cbias[1])
        h[pl.ds(lo, 2)] = v[: 2 * W].reshape(2, W, C)
        h[pl.ds(hi, 2)] = v[2 * W :].reshape(2, W, C)

        @pl.when(b == 0)
        def _():
            ysend[0] = v[:W].astype(BF16)
            ysend[1] = v[3 * W :].astype(BF16)
            start_down(yh)
            start_up(yh)

        a, c = partial_sums(v)
        return s + a, q + c

    s, q = conv(w2, y_lines)
    copies = send_stats(2, s, q)
    scale, shift = norm_terms(2, copies, params[4], params[5])

    def y_line(r, _):
        put_line(r + 1, h[r], scale, shift, shifted=False)
        return 0

    lax.fori_loop(0, R, y_line, 0)
    halo_lines(yh, yrecv.at[0], yrecv.at[1], scale, shift, shifted=False)

    for r in range(R + 2):
        pt[r, :, 0:W] = lax.dot_general(wht[...], act[1, r], nt, preferred_element_type=F32)
    for r in range(R):
        sums = []
        for j in range(3):
            x = None
            for i in range(3):
                top = 8 * (3 * i + j)
                p = pt[r + i, top : top + 8, :]
                x = p if x is None else x + p
            sums.append(x)
        mom[8 * r : 8 * r + 8] = (
            sums[1] + pltpu.roll(sums[0], 1, 1) + pltpu.roll(sums[2], LANES - 1, 1)
        )
    means = (
        jnp.dot(quant, mom[...] + head_bias, precision=lax.Precision.HIGHEST, preferred_element_type=F32)
        + quant_bias
    )
    inside = lax.broadcasted_iota(jnp.int32, means.shape, 1) < W
    latent = jnp.where(inside, LATENT_SCALE * means, 0.0).astype(BF16)
    latsend[...] = latent
    lx[0, 16:48] = latent

    def lat_copy(k, d):
        src = {0: latsend, 1: latsend.at[pl.ds(16, 16)], -1: latsend.at[pl.ds(0, 16)]}[d]
        at = {0: pl.ds(16, 32), 1: pl.ds(0, 16), -1: pl.ds(48, 16)}[d]
        return pltpu.make_async_remote_copy(
            src_ref=src, dst_ref=lx.at[k, at],
            send_sem=lat_send.at[k, d + 1], recv_sem=lat_recv.at[k, d + 1],
            device_id={"frames": f + k, "rows": rr + d}, device_id_type=MESH,
        )

    for k, d in lat_targets():
        @pl.when(sends_to(k, d))
        def _():
            lat_copy(k, d).start()

    line16 = lax.broadcasted_iota(jnp.int32, (64, LANES), 0) // 16
    for k in range(BACK + 1):
        for d in (-1, 0, 1):
            if k or d:
                @pl.when(gets_from(k, d))
                def _():
                    lat_copy(k, d).wait_recv()
        lowest = jnp.where(has_above, 0, 1)
        highest = jnp.where(has_below, 4, 3)
        lowest = jnp.where(f >= k, lowest, 4)
        keep = (line16 >= lowest) & (line16 < highest)
        x = jnp.where(keep, lx[k].astype(F32), 0.0)
        stack = jnp.concatenate(
            [pltpu.roll(x, 1, 1), x, pltpu.roll(x, LANES - 1, 1), jnp.zeros((64, LANES), F32)],
            axis=0,
        )
        ltt[k] = jnp.transpose(stack)[:W].astype(BF16)

    finish(c_t)
    n_g = 5
    sums = [[jnp.zeros((8, T), F32), jnp.zeros((8, T), F32)] for _ in range(n_g)]
    for n in range(3):
        lhs = jnp.concatenate(
            [
                jnp.concatenate([ltt[g + 2], ltt[g + 1], ltt[g]], axis=1)
                for g in range(n_g)
            ],
            axis=0,
        )
        acc = jnp.dot(lhs, wb[n], preferred_element_type=F32)
        for g in range(n_g):
            for m in range(4):
                v = acc[W * g : W * g + W, T * m : T * m + T] + tparams[0]
                t0s[g, 4 * n + m] = v
                if 2 <= 4 * n + m < R + 2:
                    a, c = partial_sums(v)
                    sums[g][0] += a
                    sums[g][1] += c

    def send_time_stats(e, sums):
        for i, (s, q) in enumerate(sums):
            tstbuf[e, rr, 2 * i : 2 * i + 1] = jnp.sum(s, axis=0, keepdims=True)
            tstbuf[e, rr, 2 * i + 1 : 2 * i + 2] = jnp.sum(q, axis=0, keepdims=True)
        copies = stat_copies(tstbuf.at[e], 3 + e)
        begin(copies)
        return copies

    def time_terms(e, copies, count, gain, shift):
        finish(copies)
        total = tstbuf[e, 0]
        for r in range(1, n_rows):
            total = total + tstbuf[e, r]
        total = lane_group_sum(total, T // GROUPS) * (1.0 / (n_rows * R * W * (T // GROUPS)))
        terms = []
        for i in range(count):
            mean = total[2 * i : 2 * i + 1]
            var = jnp.maximum(total[2 * i + 1 : 2 * i + 2] - mean * mean, 0.0)
            scale = lax.rsqrt(var + EPS) * gain
            terms.append((0.5 * scale, 0.5 * (shift - mean * scale)))
        return terms

    def time_lines(src, dst, n_lines, margin, terms):
        def line(n, _):
            at = R * rr + n - margin
            in_frame = jnp.logical_and(at >= 0, at < n_rows * R)
            for g, (scale, shift) in enumerate(terms):
                ok = jnp.logical_and(in_frame, f >= g)
                a = half_silu(src[g, n], scale, shift)
                a = jnp.where(ok, a, 0.0)
                for j, x in enumerate(column_shifts(a)):
                    dst[g, n, :, T * j : T * j + T] = x
            return 0

        lax.fori_loop(0, n_lines, line, 0)

    def pair_sums(src, weight, g, pairs):
        acc = None
        for t in range(3):
            for i in range(4):
                lhs = jnp.concatenate([src[g + 2 - t, 2 * p + i] for p in range(pairs)], axis=0)
                d = jnp.dot(lhs, weight[t, i], preferred_element_type=F32)
                acc = d if acc is None else acc + d
        return acc

    copies = send_time_stats(0, sums)
    terms = time_terms(0, copies, n_g, tparams[1], tparams[2])
    time_lines(t0s, b1, R + 4, 2, terms)

    sums = []
    for g in range(3):
        acc = pair_sums(b1, w1r, g, R // 2 + 1)
        s = jnp.zeros((8, T), F32)
        q = jnp.zeros((8, T), F32)
        for p in range(R // 2 + 1):
            for half in range(2):
                v = acc[W * p : W * p + W, T * half : T * half + T]
                t1s[g, 2 * p + half] = v
                if 1 <= 2 * p + half < R + 1:
                    a, c = partial_sums(v)
                    s += a
                    q += c
        sums.append((s, q))
    copies = send_time_stats(1, sums)
    terms = time_terms(1, copies, 3, tparams[3], tparams[4])
    time_lines(t1s, b2, R + 2, 1, terms)

    acc = pair_sums(b2, w2r, 0, R // 2)
    for p in range(R // 2):
        for half in range(2):
            v = acc[W * p : W * p + W, T * half : T * half + T] + tparams[5]
            outv[2 * p + half] = (t0s[0, 2 * p + half + 2] + v).astype(BF16)
    c_out = local(outv, out, 0)
    c_out.start()
    end_sends(vh)
    end_sends(hh)
    end_sends(yh)
    for k, d in lat_targets():
        @pl.when(sends_to(k, d))
        def _():
            lat_copy(k, d).wait_send()
    c_out.wait()


def body(
    video, norm1_gain, norm1_shift, conv1_weight, conv1_bias, norm2_gain, norm2_shift,
    conv2_weight, conv2_bias, out_gain, out_shift, out_weight, out_bias, quant_weight,
    quant_bias, time_in_weight, time_in_bias, tnorm1_gain, tnorm1_shift, time1_weight,
    tnorm2_gain, tnorm2_shift, time2_weight, time2_bias, *, n_frames, n_rows,
):
    tile = lambda a: a.reshape(4, 128)
    flat = lambda a: a.reshape(1, -1)
    args = (
        video.reshape(R, W, C),
        tile(norm1_gain), tile(norm1_shift), conv1_weight.reshape(9, C, C), flat(conv1_bias),
        tile(norm2_gain), tile(norm2_shift), conv2_weight.reshape(9, C, C), flat(conv2_bias),
        tile(out_gain), tile(out_shift), out_weight.transpose(0, 1, 3, 2).reshape(72, C), flat(out_bias),
        quant_weight.T, flat(quant_bias), time_in_weight, flat(time_in_bias),
        flat(tnorm1_gain), flat(tnorm1_shift), time1_weight.reshape(3, 3, 3 * T, T),
        flat(tnorm2_gain), flat(tnorm2_shift), time2_weight.reshape(3, 3, 3 * T, T),
        flat(time2_bias),
    )
    vmem = lambda *shape, dtype=BF16: pltpu.VMEM(shape, dtype)
    dma = pltpu.SemaphoreType.DMA
    result = pl.pallas_call(
        functools.partial(kernel, n_frames, n_rows),
        out_shape=jax.ShapeDtypeStruct((R, W, T), BF16),
        in_specs=[pl.BlockSpec(memory_space=pl.ANY)] * len(args),
        out_specs=pl.BlockSpec(memory_space=pl.ANY),
        scratch_shapes=[
            vmem(R + 2, W, C),
            vmem(9, C, C),
            vmem(9, C, C),
            vmem(3, R + 2, W, C),
            vmem(R, W, C, dtype=F32),
            vmem(2, W, C),
            vmem(2, W, C),
            vmem(2, W, C),
            vmem(2, W, C),
            vmem(6, 4, 128, dtype=F32),
            vmem(2, 1, C, dtype=F32),
            vmem(6, 1, T, dtype=F32),
            vmem(1, 8, dtype=F32),
            vmem(4, 8, dtype=F32),
            vmem(1, 4, dtype=F32),
            vmem(3, 3, 3, 4, T),
            vmem(72, C),
            vmem(R + 2, 72, LANES, dtype=F32),
            vmem(8 * R, LANES, dtype=F32),
            vmem(256, 12 * T, dtype=F32),
            vmem(3, 768, 4 * T),
            vmem(3, 4, 3 * T, 2 * T),
            vmem(3, 4, 3 * T, 2 * T),
            vmem(3, n_rows, 8, 128, dtype=F32),
            vmem(2, n_rows, 16, 128, dtype=F32),
            vmem(4 * R, LANES),
            vmem(BACK + 1, 64, LANES),
            vmem(BACK + 1, W, 256),
            vmem(5, R + 4, W, T, dtype=F32),
            vmem(5, R + 4, W, 3 * T),
            vmem(3, R + 2, W, T, dtype=F32),
            vmem(3, R + 2, W, 3 * T),
            vmem(R, W, T),
            dma((26,)),
            dma((4,)),
            dma((4,)),
            dma((4,)),
            dma((5, 2, n_rows - 1)),
            dma((BACK + 1, 3)),
            dma((BACK + 1, 3)),
        ],
        compiler_params=pltpu.CompilerParams(
            collective_id=0, has_side_effects=True, vmem_limit_bytes=62 * 1024 * 1024
        ),
        name="encoder_window",
    )(*args)
    return result[None]


def solution(mesh):
    step = functools.partial(body, n_frames=mesh.shape["frames"], n_rows=mesh.shape["rows"])
    return jax.shard_map(
        step,
        mesh=mesh,
        in_specs=(P("frames", "rows", None, None),) + (P(),) * 23,
        out_specs=P("frames", "rows", None, None),
        check_vma=False,
    )
```

profile of v0, /device:TPU:17, one launch (start us, length us, event | category | flops | bytes accessed | tf_op | source)
XLA Modules:
  0.0 71.9 jit_solution(3575901151987579274)
XLA Ops:
  0.0 70.2 %encoder_window.1 = bf16[8,160,128]{2,1,0:T(8,128)(2,1)} custom-call(bf16[8,160,512]{2,1,0:T(8,128)(2,1)} %bitcast.29, f32[4,128]{1,0:T(4,128)} %bitcast.33, f32[4,128]{1,0:T(4,128)} %bitcast.34, bf16[9,512,512]{2,1,0:T(8,128)(2,1)} %bitcast.26, f32[1,512]{1,0:T(1,128)} %bitcast.35, f32[4,128]{1,0:T(4,128)} %bitcast.36, f32[4,128]{1,0:T(4,128)} %bitcast.37, ...), custom_call_target="tpu_custom_call" | custom-call | tf_op jit(solution)/shard_map/encoder_window/pallas_call | solution.py:556
  70.2 1.7 %copy.26 = bf16[1,8,160,128]{3,2,1,0:T(8,128)(2,1)} copy(bf16[1,8,160,128]{3,2,1,0:T(8,128)(2,1)} %bitcast.28) | data formatting | bytes 655360
where the time goes:
time: 72.9 us; the launch traced here: 71.9 us
  Pallas kernels  70.2 us (96%)
  local copies, waits for them, and re-layouts  1.72 us (2%)
    pallas_call x1, Pallas kernels, body(): pl.pallas_call(functools.partial(kernel, n_frames, n_rows), out_shape=jax...  70.2 us
    unnamed x1, local copies, waits for them, and re-layouts  1.72 us

commit v1 on v0

--- a/solution.py
+++ b/solution.py
@@ -15,6 +15,7 @@
 W = 160
 C = 512
 T = 128
+HALF = C // 2
 LANES = 256
 BACK = 6
 
@@ -57,10 +58,10 @@
     video, g1, s1, cw1, cb1, g2, s2, cw2, cb2, g3, s3, ow, ob, qw, qb,
     tiw, tib, tg1, ts1, tw1, tg2, ts2, tw2, tb2,
     out,
-    vid, w1, w2, act, h, hsend, hrecv, ysend, yrecv,
+    vid, w1, w2, act, h, yp, hsend, hrecv, ysend, yrecv,
     params, cbias, tparams, obv, qwv, qbv, tiwv,
     wht, pt, mom, wbf, wb, w1r, w2r,
-    stbuf, tstbuf, latsend, lx, ltt, t0s, b1, t1s, b2, outv,
+    stbuf, tstbuf, latsend, lx, ltt, t0s, b1, t1s, b2, facc,
     in_sem, vh_sem, hh_sem, yh_sem, st_sem, lat_send, lat_recv,
 ):
     f = lax.axis_index("frames")
@@ -70,7 +71,7 @@
         return pltpu.make_async_copy(src, dst, in_sem.at[k])
 
     c_vid = local(video, vid.at[pl.ds(1, R)], 0)
-    c_w1 = local(cw1, w1, 1)
+    c_w1 = [local(cw1.at[:, :, pl.ds(HALF * i, HALF)], w1.at[i], (1, 26)[i]) for i in range(2)]
     c_w2 = local(cw2, w2, 2)
     c_par = [local(a, params.at[i], 3 + i) for i, a in enumerate((g1, s1, g2, s2, g3, s3))]
     c_cb = [local(a, cbias.at[i], 9 + i) for i, a in enumerate((cb1, cb2))]
@@ -114,6 +115,8 @@
         return ok
 
     c_vid.start()
+    stbuf[...] = jnp.zeros(stbuf.shape, F32)
+    tstbuf[...] = jnp.zeros(tstbuf.shape, F32)
     barrier = pltpu.get_barrier_semaphore()
     for d in range(1, n_rows):
         pl.semaphore_signal(
@@ -157,35 +160,37 @@
     def send_stats(e, s, q):
         s = jnp.sum(s, axis=0, keepdims=True)
         q = jnp.sum(q, axis=0, keepdims=True)
-        for t in range(C // 128):
+        tiles = s.shape[1] // 128
+        for t in range(tiles):
             stbuf[e, rr, t : t + 1, :] = s[:, 128 * t : 128 * t + 128]
-            stbuf[e, rr, 4 + t : 5 + t, :] = q[:, 128 * t : 128 * t + 128]
+            stbuf[e, rr, tiles + t : tiles + t + 1, :] = q[:, 128 * t : 128 * t + 128]
         copies = stat_copies(stbuf.at[e], e)
         begin(copies)
         return copies
 
     def norm_terms(e, copies, gain, shift):
         finish(copies)
+        tiles = gain.shape[0]
         total = stbuf[e, 0]
         for r in range(1, n_rows):
             total = total + stbuf[e, r]
         total = lane_group_sum(total, C // GROUPS) * (1.0 / (n_rows * R * W * (C // GROUPS)))
-        mean = total[0:4]
-        var = jnp.maximum(total[4:8] - mean * mean, 0.0)
+        mean = total[0:tiles]
+        var = jnp.maximum(total[tiles : 2 * tiles] - mean * mean, 0.0)
         scale = lax.rsqrt(var + EPS) * gain
         shift = shift - mean * scale
-        wide = lambda x: jnp.concatenate([x[t : t + 1] for t in range(C // 128)], axis=1) * 0.5
+        wide = lambda x: jnp.concatenate([x[t : t + 1] for t in range(tiles)], axis=1) * 0.5
         return wide(scale), wide(shift)
 
-    def put_line(line, v, scale, shift, shifted=True):
+    def put_line(line, v, scale, shift, halves=(0, 1), shifted=True):
         a = half_silu(v, scale, shift)
-        if shifted:
-            for j, x in enumerate(column_shifts(a)):
-                act[j, line] = x
-        else:
-            act[1, line] = a.astype(BF16)
-
-    def halo_lines(copies, above, below, scale, shift, shifted=True):
+        taps = column_shifts(a) if shifted else (None, a.astype(BF16), None)
+        for j, x in enumerate(taps):
+            if x is not None:
+                for n, half in enumerate(halves):
+                    act[half, j, line] = x[:, HALF * n : HALF * n + HALF]
+
+    def halo_lines(copies, above, below, scale, shift, halves=(0, 1), shifted=True):
         taps = range(3) if shifted else (1,)
         for has, copy, ref, line in (
             (has_above, copies[0], above, 0),
@@ -194,12 +199,13 @@
             @pl.when(has)
             def _():
                 copy.wait_recv()
-                put_line(line, ref[...].astype(F32), scale, shift, shifted)
+                put_line(line, ref[...].astype(F32), scale, shift, halves, shifted)
 
             @pl.when(jnp.logical_not(has))
             def _():
-                for j in taps:
-                    act[j, line] = jnp.zeros((W, C), BF16)
+                for half in halves:
+                    for j in taps:
+                        act[half, j, line] = jnp.zeros((W, HALF), BF16)
 
     def start_down(copies):
         @pl.when(has_below)
@@ -220,7 +226,7 @@
         def _():
             copies[1].wait_send()
 
-    def conv(weight, finish_line):
+    def conv(lhs_of, weight_of, width, finish_lines):
         def block(b, carry):
             s, q = carry
             lo = 2 * b
@@ -228,23 +234,19 @@
             acc = None
             for i in range(3):
                 for j in range(3):
-                    lhs = jnp.concatenate(
-                        [
-                            act[j, pl.ds(lo + i, 2)].reshape(2 * W, C),
-                            act[j, pl.ds(hi + i, 2)].reshape(2 * W, C),
-                        ],
-                        axis=0,
-                    )
-                    d = jnp.dot(lhs, weight[3 * i + j], preferred_element_type=F32)
+                    lhs = jnp.concatenate([lhs_of(j, lo + i), lhs_of(j, hi + i)], axis=0)
+                    d = jnp.dot(lhs, weight_of(3 * i + j), preferred_element_type=F32)
                     acc = d if acc is None else acc + d
-            return finish_line(b, lo, hi, acc, s, q)
-
-        zero = jnp.zeros((8, C), F32)
+            return finish_lines(b, lo, hi, acc, s, q)
+
+        zero = jnp.zeros((8, width), F32)
         return lax.fori_loop(0, 2, block, (zero, zero))
 
-    tstbuf[...] = jnp.zeros(tstbuf.shape, F32)
+    def two_lines(half, j, line):
+        return act[half, j, pl.ds(line, 2)].reshape(2 * W, HALF)
+
     c_vid.wait()
-    c_w1.start()
+    begin(c_w1)
 
     def video_sums(r, carry):
         s, q = carry
@@ -286,28 +288,89 @@
 
     lax.fori_loop(0, R, video_line, 0)
     halo_lines(vh, vid.at[0], vid.at[R + 1], scale, shift)
-    c_w1.wait()
-
-    hh = halo(hsend.at[1], hsend.at[0], hrecv.at[0], hrecv.at[1], hh_sem)
-
-    def h_lines(b, lo, hi, acc, s, q):
-        v = acc + cbias[0]
-        h[pl.ds(lo, 2)] = v[: 2 * W].reshape(2, W, C)
-        h[pl.ds(hi, 2)] = v[2 * W :].reshape(2, W, C)
+    finish(c_w1)
+
+    hh = [halo(hsend.at[i, 1], hsend.at[i, 0], hrecv.at[i, 0], hrecv.at[i, 1], hh_sem.at[i]) for i in range(2)]
+    h_copies = []
+    for half in range(2):
+
+        def h_lines(b, lo, hi, acc, s, q):
+            v = acc + cbias[0, :, HALF * half : HALF * half + HALF]
+            h[half, pl.ds(lo, 2)] = v[: 2 * W].reshape(2, W, HALF)
+            h[half, pl.ds(hi, 2)] = v[2 * W :].reshape(2, W, HALF)
+
+            @pl.when(b == 0)
+            def _():
+                hsend[half, 0] = v[:W].astype(BF16)
+                hsend[half, 1] = v[3 * W :].astype(BF16)
+                start_down(hh[half])
+                start_up(hh[half])
+
+            a, c = partial_sums(v)
+            return s + a, q + c
+
+        s, q = conv(
+            lambda j, line: jnp.concatenate([two_lines(0, j, line), two_lines(1, j, line)], axis=1),
+            lambda tap: w1[half, tap],
+            HALF,
+            h_lines,
+        )
+        h_copies.append(send_stats(1 + half, s, q))
+
+    def h_norm(half):
+        scale, shift = norm_terms(
+            1 + half, h_copies[half], params[2, 2 * half : 2 * half + 2], params[3, 2 * half : 2 * half + 2]
+        )
+
+        def h_line(r, _):
+            put_line(r + 1, h[half, r], scale, shift, (half,))
+            return 0
+
+        lax.fori_loop(0, R, h_line, 0)
+        halo_lines(hh[half], hrecv.at[half, 0], hrecv.at[half, 1], scale, shift, (half,))
+
+    h_norm(0)
+    c_w2.wait()
+
+    yh = halo(ysend.at[1], ysend.at[0], yrecv.at[0], yrecv.at[1], yh_sem)
+
+    def y_part(b, lo, hi, acc, s, q):
+        res = jnp.concatenate(
+            [vid[pl.ds(lo + 1, 2)].reshape(2 * W, C), vid[pl.ds(hi + 1, 2)].reshape(2 * W, C)],
+            axis=0,
+        )
+        v = res.astype(F32) + (acc + cbias[1])
+        yp[pl.ds(lo, 2)] = v[: 2 * W].reshape(2, W, C)
+        yp[pl.ds(hi, 2)] = v[2 * W :].reshape(2, W, C)
+        return s, q
+
+    def y_lines(b, lo, hi, acc, s, q):
+        part = jnp.concatenate(
+            [yp[pl.ds(lo, 2)].reshape(2 * W, C), yp[pl.ds(hi, 2)].reshape(2 * W, C)], axis=0
+        )
+        v = part + acc
+        for half in range(2):
+            x = v[:, HALF * half : HALF * half + HALF]
+            h[half, pl.ds(lo, 2)] = x[: 2 * W].reshape(2, W, HALF)
+            h[half, pl.ds(hi, 2)] = x[2 * W :].reshape(2, W, HALF)
 
         @pl.when(b == 0)
         def _():
-            hsend[0] = v[:W].astype(BF16)
-            hsend[1] = v[3 * W :].astype(BF16)
-            start_down(hh)
-            start_up(hh)
+            ysend[0] = v[:W].astype(BF16)
+            ysend[1] = v[3 * W :].astype(BF16)
+            start_down(yh)
+            start_up(yh)
 
         a, c = partial_sums(v)
         return s + a, q + c
 
-    s, q = conv(w1, h_lines)
-    copies = send_stats(1, s, q)
-
+    conv(lambda j, line: two_lines(0, j, line), lambda tap: w2[tap, 0:HALF], C, y_part)
+
+    h_norm(1)
+
+    s, q = conv(lambda j, line: two_lines(1, j, line), lambda tap: w2[tap, HALF:C], C, y_lines)
+
+    copies = send_stats(3, s, q)
     finish([c_ow] + c_q + c_tp)
     nt = (((1,), (1,)), ((), ()))
     pt[...] = jnp.zeros(pt.shape, F32)
@@ -331,50 +394,19 @@
     for c in range(4):
         quant_bias = quant_bias + jnp.where(row4 % 4 == c, qbv[0:1, c : c + 1], 0.0)
 
-    scale, shift = norm_terms(1, copies, params[2], params[3])
-
-    def h_line(r, _):
-        put_line(r + 1, h[r], scale, shift)
-        return 0
-
-    lax.fori_loop(0, R, h_line, 0)
-    halo_lines(hh, hrecv.at[0], hrecv.at[1], scale, shift)
-    c_w2.wait()
-
-    yh = halo(ysend.at[1], ysend.at[0], yrecv.at[0], yrecv.at[1], yh_sem)
-
-    def y_lines(b, lo, hi, acc, s, q):
-        res = jnp.concatenate(
-            [vid[pl.ds(lo + 1, 2)].reshape(2 * W, C), vid[pl.ds(hi + 1, 2)].reshape(2 * W, C)],
-            axis=0,
-        )
-        v = res.astype(F32) + (acc + cbias[1])
-        h[pl.ds(lo, 2)] = v[: 2 * W].reshape(2, W, C)
-        h[pl.ds(hi, 2)] = v[2 * W :].reshape(2, W, C)
-
-        @pl.when(b == 0)
-        def _():
-            ysend[0] = v[:W].astype(BF16)
-            ysend[1] = v[3 * W :].astype(BF16)
-            start_down(yh)
-            start_up(yh)
-
-        a, c = partial_sums(v)
-        return s + a, q + c
-
-    s, q = conv(w2, y_lines)
-    copies = send_stats(2, s, q)
-    scale, shift = norm_terms(2, copies, params[4], params[5])
+    scale, shift = norm_terms(3, copies, params[4], params[5])
 
     def y_line(r, _):
-        put_line(r + 1, h[r], scale, shift, shifted=False)
+        v = jnp.concatenate([h[0, r], h[1, r]], axis=1)
+        put_line(r + 1, v, scale, shift, shifted=False)
         return 0
 
     lax.fori_loop(0, R, y_line, 0)
     halo_lines(yh, yrecv.at[0], yrecv.at[1], scale, shift, shifted=False)
 
     for r in range(R + 2):
-        pt[r, :, 0:W] = lax.dot_general(wht[...], act[1, r], nt, preferred_element_type=F32)
+        line = jnp.concatenate([act[0, 1, r], act[1, 1, r]], axis=1)
+        pt[r, :, 0:W] = lax.dot_general(wht[...], line, nt, preferred_element_type=F32)
     for r in range(R):
         sums = []
         for j in range(3):
@@ -411,99 +443,99 @@
             lat_copy(k, d).start()
 
     line16 = lax.broadcasted_iota(jnp.int32, (64, LANES), 0) // 16
-    for k in range(BACK + 1):
-        for d in (-1, 0, 1):
-            if k or d:
-                @pl.when(gets_from(k, d))
-                def _():
-                    lat_copy(k, d).wait_recv()
-        lowest = jnp.where(has_above, 0, 1)
-        highest = jnp.where(has_below, 4, 3)
-        lowest = jnp.where(f >= k, lowest, 4)
-        keep = (line16 >= lowest) & (line16 < highest)
+    column = lax.broadcasted_iota(jnp.int32, (W, 128), 0)
+    lowest = jnp.where(has_above, 0, 1)
+    highest = jnp.where(has_below, 4, 3)
+
+    def take_latent(k, dirs=(-1, 0, 1)):
+        for d in dirs:
+            @pl.when(gets_from(k, d))
+            def _():
+                lat_copy(k, d).wait_recv()
+        keep = (line16 >= jnp.where(f >= k, lowest, 4)) & (line16 < highest)
         x = jnp.where(keep, lx[k].astype(F32), 0.0)
-        stack = jnp.concatenate(
-            [pltpu.roll(x, 1, 1), x, pltpu.roll(x, LANES - 1, 1), jnp.zeros((64, LANES), F32)],
-            axis=0,
-        )
-        ltt[k] = jnp.transpose(stack)[:W].astype(BF16)
-
-    finish(c_t)
-    n_g = 5
-    sums = [[jnp.zeros((8, T), F32), jnp.zeros((8, T), F32)] for _ in range(n_g)]
-    for n in range(3):
-        lhs = jnp.concatenate(
-            [
-                jnp.concatenate([ltt[g + 2], ltt[g + 1], ltt[g]], axis=1)
-                for g in range(n_g)
-            ],
-            axis=0,
-        )
-        acc = jnp.dot(lhs, wb[n], preferred_element_type=F32)
-        for g in range(n_g):
-            for m in range(4):
-                v = acc[W * g : W * g + W, T * m : T * m + T] + tparams[0]
-                t0s[g, 4 * n + m] = v
-                if 2 <= 4 * n + m < R + 2:
-                    a, c = partial_sums(v)
-                    sums[g][0] += a
-                    sums[g][1] += c
-
-    def send_time_stats(e, sums):
-        for i, (s, q) in enumerate(sums):
-            tstbuf[e, rr, 2 * i : 2 * i + 1] = jnp.sum(s, axis=0, keepdims=True)
-            tstbuf[e, rr, 2 * i + 1 : 2 * i + 2] = jnp.sum(q, axis=0, keepdims=True)
-        copies = stat_copies(tstbuf.at[e], 3 + e)
-        begin(copies)
-        return copies
-
-    def time_terms(e, copies, count, gain, shift):
-        finish(copies)
+        x = jnp.transpose(jnp.concatenate([x, jnp.zeros((64, LANES), F32)], axis=0))[:W]
+        left = jnp.where(column == 0, 0.0, pltpu.roll(x, 1, 0))
+        right = jnp.where(column == W - 1, 0.0, pltpu.roll(x, W - 1, 0))
+        ltt[k, :, 0:128] = (left + pltpu.roll(x, 64, 1)).astype(BF16)
+        ltt[k, :, 128:256] = right.astype(BF16)
+
+    def send_time_stats(e, s, q):
+        tstbuf[e, rr, 0:1] = jnp.sum(s, axis=0, keepdims=True)
+        tstbuf[e, rr, 1:2] = jnp.sum(q, axis=0, keepdims=True)
+        begin(stat_copies(tstbuf.at[e], 4 + e))
+
+    def time_terms(e, gain, shift):
+        finish(stat_copies(tstbuf.at[e], 4 + e))
         total = tstbuf[e, 0]
         for r in range(1, n_rows):
             total = total + tstbuf[e, r]
         total = lane_group_sum(total, T // GROUPS) * (1.0 / (n_rows * R * W * (T // GROUPS)))
-        terms = []
-        for i in range(count):
-            mean = total[2 * i : 2 * i + 1]
-            var = jnp.maximum(total[2 * i + 1 : 2 * i + 2] - mean * mean, 0.0)
-            scale = lax.rsqrt(var + EPS) * gain
-            terms.append((0.5 * scale, 0.5 * (shift - mean * scale)))
-        return terms
-
-    def time_lines(src, dst, n_lines, margin, terms):
-        def line(n, _):
-            at = R * rr + n - margin
-            in_frame = jnp.logical_and(at >= 0, at < n_rows * R)
-            for g, (scale, shift) in enumerate(terms):
-                ok = jnp.logical_and(in_frame, f >= g)
-                a = half_silu(src[g, n], scale, shift)
-                a = jnp.where(ok, a, 0.0)
+        mean = total[0:1]
+        var = jnp.maximum(total[1:2] - mean * mean, 0.0)
+        scale = lax.rsqrt(var + EPS) * gain
+        return 0.5 * scale, 0.5 * (shift - mean * scale)
+
+    def time_lines(src, dst, g, n_lines, margin, terms):
+        scale, shift = terms
+
+        def lines(m, _):
+            for n in (2 * m, 2 * m + 1):
+                at = R * rr + n - margin
+                ok = jnp.logical_and(jnp.logical_and(at >= 0, at < n_rows * R), f >= g)
+                a = jnp.where(ok, half_silu(src[g, n], scale, shift), 0.0)
                 for j, x in enumerate(column_shifts(a)):
                     dst[g, n, :, T * j : T * j + T] = x
             return 0
 
-        lax.fori_loop(0, n_lines, line, 0)
-
-    def pair_sums(src, weight, g, pairs):
-        acc = None
-        for t in range(3):
-            for i in range(4):
-                lhs = jnp.concatenate([src[g + 2 - t, 2 * p + i] for p in range(pairs)], axis=0)
-                d = jnp.dot(lhs, weight[t, i], preferred_element_type=F32)
-                acc = d if acc is None else acc + d
-        return acc
-
-    copies = send_time_stats(0, sums)
-    terms = time_terms(0, copies, n_g, tparams[1], tparams[2])
-    time_lines(t0s, b1, R + 4, 2, terms)
-
-    sums = []
-    for g in range(3):
-        acc = pair_sums(b1, w1r, g, R // 2 + 1)
+        lax.fori_loop(0, n_lines // 2, lines, 0)
+
+    def pair_lines(src, g, i, pairs):
+        return jnp.concatenate([src[g, 2 * p + i] for p in range(pairs)], axis=0)
+
+    take_latent(0, (-1, 1))
+    take_latent(1)
+
+    def t0_frame(g, _):
+        take_latent(g + 2)
+        lhs = jnp.concatenate([ltt[g + 2], ltt[g + 1], ltt[g]], axis=1)
         s = jnp.zeros((8, T), F32)
         q = jnp.zeros((8, T), F32)
-        for p in range(R // 2 + 1):
+        for n in range(3):
+            acc = jnp.dot(lhs, wb[n], preferred_element_type=F32)
+            for m in range(4):
+                v = acc[:, T * m : T * m + T] + tparams[0]
+                t0s[g, 4 * n + m] = v
+                if 2 <= 4 * n + m < R + 2:
+                    a, c = partial_sums(v)
+                    s += a
+                    q += c
+        send_time_stats(g, s, q)
+        return 0
+
+    lax.fori_loop(0, 5, t0_frame, 0)
+
+    finish(c_t)
+
+    def b1_frame(g):
+        time_lines(t0s, b1, g, R + 4, 2, time_terms(g, tparams[1], tparams[2]))
+
+    def b1_first(g, _):
+        b1_frame(g)
+        return 0
+
+    lax.fori_loop(0, 2, b1_first, 0)
+
+    def t1_frame(g, _):
+        b1_frame(g + 2)
+        pairs = R // 2 + 1
+        lhs = jnp.concatenate(
+            [pair_lines(b1, g + 2 - t, i, pairs) for t in range(3) for i in range(4)], axis=1
+        )
+        acc = jnp.dot(lhs, w1r[...].reshape(12 * 3 * T, 2 * T), preferred_element_type=F32)
+        s = jnp.zeros((8, T), F32)
+        q = jnp.zeros((8, T), F32)
+        for p in range(pairs):
             for half in range(2):
                 v = acc[W * p : W * p + W, T * half : T * half + T]
                 t1s[g, 2 * p + half] = v
@@ -511,26 +543,36 @@
                     a, c = partial_sums(v)
                     s += a
                     q += c
-        sums.append((s, q))
-    copies = send_time_stats(1, sums)
-    terms = time_terms(1, copies, 3, tparams[3], tparams[4])
-    time_lines(t1s, b2, R + 2, 1, terms)
-
-    acc = pair_sums(b2, w2r, 0, R // 2)
+        send_time_stats(5 + g, s, q)
+        return 0
+
+    lax.fori_loop(0, 3, t1_frame, 0)
+
     for p in range(R // 2):
         for half in range(2):
-            v = acc[W * p : W * p + W, T * half : T * half + T] + tparams[5]
-            outv[2 * p + half] = (t0s[0, 2 * p + half + 2] + v).astype(BF16)
-    c_out = local(outv, out, 0)
-    c_out.start()
+            facc[W * p : W * p + W, T * half : T * half + T] = t0s[0, 2 * p + half + 2] + tparams[5]
+
+    def feature_frame(g, _):
+        time_lines(t1s, b2, g, R + 2, 1, time_terms(5 + g, tparams[3], tparams[4]))
+        lhs = jnp.concatenate([pair_lines(b2, g, i, R // 2) for i in range(4)], axis=1)
+        facc[...] += jnp.dot(
+            lhs, w2r[2 - g].reshape(4 * 3 * T, 2 * T), preferred_element_type=F32
+        )
+        return 0
+
+    lax.fori_loop(0, 3, feature_frame, 0)
+
+    for p in range(R // 2):
+        for half in range(2):
+            out[2 * p + half] = facc[W * p : W * p + W, T * half : T * half + T].astype(BF16)
     end_sends(vh)
-    end_sends(hh)
+    end_sends(hh[0])
+    end_sends(hh[1])
     end_sends(yh)
     for k, d in lat_targets():
         @pl.when(sends_to(k, d))
         def _():
             lat_copy(k, d).wait_send()
-    c_out.wait()
 
 
 def body(
@@ -557,15 +599,16 @@
         functools.partial(kernel, n_frames, n_rows),
         out_shape=jax.ShapeDtypeStruct((R, W, T), BF16),
         in_specs=[pl.BlockSpec(memory_space=pl.ANY)] * len(args),
-        out_specs=pl.BlockSpec(memory_space=pl.ANY),
+        out_specs=pl.BlockSpec(memory_space=pltpu.VMEM),
         scratch_shapes=[
             vmem(R + 2, W, C),
+            vmem(2, 9, C, HALF),
             vmem(9, C, C),
-            vmem(9, C, C),
-            vmem(3, R + 2, W, C),
+            vmem(2, 3, R + 2, W, HALF),
+            vmem(2, R, W, HALF, dtype=F32),
             vmem(R, W, C, dtype=F32),
-            vmem(2, W, C),
-            vmem(2, W, C),
+            vmem(2, 2, W, HALF),
+            vmem(2, 2, W, HALF),
             vmem(2, W, C),
             vmem(2, W, C),
             vmem(6, 4, 128, dtype=F32),
@@ -582,8 +625,8 @@
             vmem(3, 768, 4 * T),
             vmem(3, 4, 3 * T, 2 * T),
             vmem(3, 4, 3 * T, 2 * T),
-            vmem(3, n_rows, 8, 128, dtype=F32),
-            vmem(2, n_rows, 16, 128, dtype=F32),
+            vmem(4, n_rows, 8, 128, dtype=F32),
+            vmem(8, n_rows, 8, 128, dtype=F32),
             vmem(4 * R, LANES),
             vmem(BACK + 1, 64, LANES),
             vmem(BACK + 1, W, 256),
@@ -591,17 +634,17 @@
             vmem(5, R + 4, W, 3 * T),
             vmem(3, R + 2, W, T, dtype=F32),
             vmem(3, R + 2, W, 3 * T),
-            vmem(R, W, T),
-            dma((26,)),
+            vmem(R // 2 * W, 2 * T, dtype=F32),
+            dma((28,)),
             dma((4,)),
+            dma((2, 4)),
             dma((4,)),
-            dma((4,)),
-            dma((5, 2, n_rows - 1)),
+            dma((12, 2, n_rows - 1)),
             dma((BACK + 1, 3)),
             dma((BACK + 1, 3)),
         ],
         compiler_params=pltpu.CompilerParams(
-            collective_id=0, has_side_effects=True, vmem_limit_bytes=62 * 1024 * 1024
+            collective_id=0, has_side_effects=True, vmem_limit_bytes=60 * 1024 * 1024
         ),
         name="encoder_window",
     )(*args)

time: 72.9 us -> 60.4 us (0.83); the launches traced: 71.9 us -> 60.3 us
  Pallas kernels: 70.2 us -> 58.5 us
    pallas_call x1, Pallas kernels: 70.2 us -> 58.5 us  [body(): pl.pallas_call(functools.partial(kernel, n_frames, n_rows), out_shape=jax...]
where the time goes in v1:
time: 60.4 us; the launch traced here: 60.3 us
  Pallas kernels  58.5 us (97%)
  local copies, waits for them, and re-layouts  1.72 us (3%)
    pallas_call x1, Pallas kernels, body(): pl.pallas_call(functools.partial(kernel, n_frames, n_rows), out_shape=jax...  58.5 us
    unnamed x1, local copies, waits for them, and re-layouts  1.72 us

profile of v1, /device:TPU:17, one launch (start us, length us, event | category | flops | bytes accessed | tf_op | source)
XLA Modules:
  0.0 60.3 jit_solution(13356678968841360399)
XLA Ops:
  0.0 58.5 %encoder_window.1 = bf16[8,160,128]{2,1,0:T(8,128)(2,1)} custom-call(bf16[8,160,512]{2,1,0:T(8,128)(2,1)} %bitcast.29, f32[4,128]{1,0:T(4,128)} %bitcast.33, f32[4,128]{1,0:T(4,128)} %bitcast.34, bf16[9,512,512]{2,1,0:T(8,128)(2,1)} %bitcast.26, f32[1,512]{1,0:T(1,128)} %bitcast.35, f32[4,128]{1,0:T(4,128)} %bitcast.36, f32[4,128]{1,0:T(4,128)} %bitcast.37, ...), custom_call_target="tpu_custom_call" | custom-call | tf_op jit(solution)/shard_map/encoder_window/pallas_call | solution.py:598
  58.5 1.7 %copy.26 = bf16[1,8,160,128]{3,2,1,0:T(8,128)(2,1)} copy(bf16[1,8,160,128]{3,2,1,0:T(8,128)(2,1)} %bitcast.28) | data formatting | bytes 655360

commit v2 on v1

--- a/solution.py
+++ b/solution.py
@@ -17,6 +17,7 @@
 T = 128
 HALF = C // 2
 LANES = 256
+SLOTS = 80
 BACK = 6
 
 MESH = pl.DeviceIdType.MESH
@@ -36,15 +37,25 @@
 
 
 def column_shifts(a):
-    col = lax.broadcasted_iota(jnp.int32, a.shape, 0)
-    left = jnp.where(col == 0, 0.0, pltpu.roll(a, 1, 0))
-    right = jnp.where(col == W - 1, 0.0, pltpu.roll(a, W - 1, 0))
+    row = lax.broadcasted_iota(jnp.int32, (8, a.shape[1]), 0)
+    left = pltpu.roll(a, 1, 0)
+    left = jnp.concatenate([jnp.where(row == 0, 0.0, left[:8]), left[8:]], axis=0)
+    right = pltpu.roll(a, W - 1, 0)
+    right = jnp.concatenate([right[: W - 8], jnp.where(row == 7, 0.0, right[W - 8 :])], axis=0)
     return left.astype(BF16), a.astype(BF16), right.astype(BF16)
 
 
 def half_silu(v, scale, shift):
     w = v * scale + shift
     return w * jnp.tanh(w) + w
+
+
+def packed_row(line):
+    if line < 0:
+        return 5 * (line + 3)
+    if line < R:
+        return 16 + 5 * line
+    return 64 + 5 * (line - R)
 
 
 def partial_sums(v):
@@ -74,7 +85,11 @@
     c_w1 = [local(cw1.at[:, :, pl.ds(HALF * i, HALF)], w1.at[i], (1, 26)[i]) for i in range(2)]
     c_w2 = local(cw2, w2, 2)
     c_par = [local(a, params.at[i], 3 + i) for i, a in enumerate((g1, s1, g2, s2, g3, s3))]
-    c_cb = [local(a, cbias.at[i], 9 + i) for i, a in enumerate((cb1, cb2))]
+    c_cb = [
+        local(a.at[:, pl.ds(HALF * n, HALF)], cbias.at[i, n], (9, 27)[n] + i)
+        for i, a in enumerate((cb1, cb2))
+        for n in range(2)
+    ]
     c_tp = [local(a, tparams.at[i], 11 + i) for i, a in enumerate((tib, tg1, ts1, tg2, ts2, tb2))]
     c_ow = local(ow, wht, 17)
     c_q = [local(ob, obv, 18), local(qw, qwv, 19), local(qb, qbv, 20)]
@@ -274,7 +289,7 @@
             for i in range(3):
                 piece = tiwv[t, i, j].astype(F32)
                 for n in range(R + 4):
-                    top = 64 * j + 4 * (n + 1 + i)
+                    top = SLOTS * j + packed_row(n + i - 3)
                     wbf[top : top + 4, T * n : T * n + T] = piece
         for n in range(3):
             wb[n, 256 * t : 256 * t + 256] = wbf[:, 512 * n : 512 * n + 512].astype(BF16)
@@ -291,35 +306,33 @@
     finish(c_w1)
 
     hh = [halo(hsend.at[i, 1], hsend.at[i, 0], hrecv.at[i, 0], hrecv.at[i, 1], hh_sem.at[i]) for i in range(2)]
-    h_copies = []
-    for half in range(2):
-
-        def h_lines(b, lo, hi, acc, s, q):
-            v = acc + cbias[0, :, HALF * half : HALF * half + HALF]
-            h[half, pl.ds(lo, 2)] = v[: 2 * W].reshape(2, W, HALF)
-            h[half, pl.ds(hi, 2)] = v[2 * W :].reshape(2, W, HALF)
-
-            @pl.when(b == 0)
-            def _():
-                hsend[half, 0] = v[:W].astype(BF16)
-                hsend[half, 1] = v[3 * W :].astype(BF16)
-                start_down(hh[half])
-                start_up(hh[half])
-
-            a, c = partial_sums(v)
-            return s + a, q + c
-
-        s, q = conv(
-            lambda j, line: jnp.concatenate([two_lines(0, j, line), two_lines(1, j, line)], axis=1),
-            lambda tap: w1[half, tap],
-            HALF,
-            h_lines,
-        )
-        h_copies.append(send_stats(1 + half, s, q))
+
+    def h_half(half, _):
+        acc = None
+        for i in range(3):
+            for j in range(3):
+                lhs = jnp.concatenate(
+                    [act[n, j, i : i + R].reshape(R * W, HALF) for n in range(2)], axis=1
+                )
+                d = jnp.dot(lhs, w1[half, 3 * i + j], preferred_element_type=F32)
+                acc = d if acc is None else acc + d
+        v = acc + cbias[0, half]
+        h[half] = v.reshape(R, W, HALF)
+        hsend[half, 0] = v[:W].astype(BF16)
+        hsend[half, 1] = v[R * W - W :].astype(BF16)
+        copies = halo(
+            hsend.at[half, 1], hsend.at[half, 0], hrecv.at[half, 0], hrecv.at[half, 1], hh_sem.at[half]
+        )
+        send_stats(1 + half, *partial_sums(v))
+        start_down(copies)
+        start_up(copies)
+        return 0
+
+    lax.fori_loop(0, 2, h_half, 0)
 
     def h_norm(half):
         scale, shift = norm_terms(
-            1 + half, h_copies[half], params[2, 2 * half : 2 * half + 2], params[3, 2 * half : 2 * half + 2]
+            1 + half, stat_copies(stbuf.at[1 + half], 1 + half), params[2, 2 * half : 2 * half + 2], params[3, 2 * half : 2 * half + 2]
         )
 
         def h_line(r, _):
@@ -339,7 +352,7 @@
             [vid[pl.ds(lo + 1, 2)].reshape(2 * W, C), vid[pl.ds(hi + 1, 2)].reshape(2 * W, C)],
             axis=0,
         )
-        v = res.astype(F32) + (acc + cbias[1])
+        v = res.astype(F32) + (acc + jnp.concatenate([cbias[1, 0], cbias[1, 1]], axis=1))
         yp[pl.ds(lo, 2)] = v[: 2 * W].reshape(2, W, C)
         yp[pl.ds(hi, 2)] = v[2 * W :].reshape(2, W, C)
         return s, q
@@ -378,21 +391,21 @@
         for dst in (w1r, w2r):
             dst[t, 3, :, 0:T] = jnp.zeros((3 * T, T), BF16)
             dst[t, 0, :, T : 2 * T] = jnp.zeros((3 * T, T), BF16)
-    row = lax.broadcasted_iota(jnp.int32, (4 * R, 8 * R), 0)
-    col = lax.broadcasted_iota(jnp.int32, (4 * R, 8 * R), 1)
-    quant = jnp.zeros((4 * R, 8 * R), F32)
+    row = lax.broadcasted_iota(jnp.int32, (48, 8 * R), 0)
+    col = lax.broadcasted_iota(jnp.int32, (48, 8 * R), 1)
+    quant = jnp.zeros((48, 8 * R), F32)
     for m in range(8):
         for c in range(4):
-            hit = (row % 4 == c) & (col % 8 == m) & (row // 4 == col // 8)
+            hit = (row % 5 == c) & (col % 8 == m) & (row // 5 == col // 8)
             quant = quant + jnp.where(hit, qwv[c : c + 1, m : m + 1], 0.0)
     row8 = lax.broadcasted_iota(jnp.int32, (8 * R, 1), 0)
-    row4 = lax.broadcasted_iota(jnp.int32, (4 * R, 1), 0)
+    row5 = lax.broadcasted_iota(jnp.int32, (48, 1), 0)
     head_bias = jnp.zeros((8 * R, 1), F32)
     for m in range(8):
         head_bias = head_bias + jnp.where(row8 % 8 == m, obv[0:1, m : m + 1], 0.0)
-    quant_bias = jnp.zeros((4 * R, 1), F32)
+    quant_bias = jnp.zeros((48, 1), F32)
     for c in range(4):
-        quant_bias = quant_bias + jnp.where(row4 % 4 == c, qbv[0:1, c : c + 1], 0.0)
+        quant_bias = quant_bias + jnp.where(row5 % 5 == c, qbv[0:1, c : c + 1], 0.0)
 
     scale, shift = norm_terms(3, copies, params[4], params[5])
 
@@ -423,16 +436,24 @@
         jnp.dot(quant, mom[...] + head_bias, precision=lax.Precision.HIGHEST, preferred_element_type=F32)
         + quant_bias
     )
-    inside = lax.broadcasted_iota(jnp.int32, means.shape, 1) < W
-    latent = jnp.where(inside, LATENT_SCALE * means, 0.0).astype(BF16)
-    latsend[...] = latent
-    lx[0, 16:48] = latent
+    means = LATENT_SCALE * means
+    row = lax.broadcasted_iota(jnp.int32, (48, 128), 0)
+    lane = lax.broadcasted_iota(jnp.int32, (48, 128), 1)
+    rest = jnp.where((lane < W - 128) & (row < 5 * R), means[:, 128:256], 0.0)
+    packed = jnp.where(row % 5 < 4, means[:, 0:128], 0.0)
+    for c in range(4):
+        moved = pltpu.roll(jnp.where(row % 5 == c, rest, 0.0), 4 - c, 0)
+        packed = packed + (pltpu.roll(moved, 32 * c, 1) if c else moved)
+    packed = jnp.where(row < 5 * R, packed, 0.0)
+    latsend[0:48] = packed.astype(BF16)
+    latsend[48:64] = pltpu.roll(packed, 48 - 25, 0)[0:16].astype(BF16)
+    lx[0, 16:64] = packed.astype(BF16)
 
     def lat_copy(k, d):
-        src = {0: latsend, 1: latsend.at[pl.ds(16, 16)], -1: latsend.at[pl.ds(0, 16)]}[d]
-        at = {0: pl.ds(16, 32), 1: pl.ds(0, 16), -1: pl.ds(48, 16)}[d]
+        src = {0: pl.ds(0, 48), 1: pl.ds(48, 16), -1: pl.ds(0, 16)}[d]
+        at = {0: pl.ds(16, 48), 1: pl.ds(0, 16), -1: pl.ds(64, 16)}[d]
         return pltpu.make_async_remote_copy(
-            src_ref=src, dst_ref=lx.at[k, at],
+            src_ref=latsend.at[src], dst_ref=lx.at[k, at],
             send_sem=lat_send.at[k, d + 1], recv_sem=lat_recv.at[k, d + 1],
             device_id={"frames": f + k, "rows": rr + d}, device_id_type=MESH,
         )
@@ -442,23 +463,33 @@
         def _():
             lat_copy(k, d).start()
 
-    line16 = lax.broadcasted_iota(jnp.int32, (64, LANES), 0) // 16
+    slot = lax.broadcasted_iota(jnp.int32, (SLOTS, 128), 0)
+    lowest = jnp.where(has_above, 0, 16)
+    highest = jnp.where(has_below, SLOTS, 64)
     column = lax.broadcasted_iota(jnp.int32, (W, 128), 0)
-    lowest = jnp.where(has_above, 0, 1)
-    highest = jnp.where(has_below, 4, 3)
+    lane = lax.broadcasted_iota(jnp.int32, (W, 128), 1)
+    lane32 = lax.broadcasted_iota(jnp.int32, (32, 128), 1)
+    fifth = lane32 < 0
+    for line in range(-3, R + 3):
+        fifth = fifth | (lane32 == packed_row(line) + 4)
 
     def take_latent(k, dirs=(-1, 0, 1)):
         for d in dirs:
             @pl.when(gets_from(k, d))
             def _():
                 lat_copy(k, d).wait_recv()
-        keep = (line16 >= jnp.where(f >= k, lowest, 4)) & (line16 < highest)
+        keep = (slot >= jnp.where(f >= k, lowest, SLOTS)) & (slot < highest)
         x = jnp.where(keep, lx[k].astype(F32), 0.0)
-        x = jnp.transpose(jnp.concatenate([x, jnp.zeros((64, LANES), F32)], axis=0))[:W]
+        x = jnp.transpose(jnp.concatenate([x, jnp.zeros((128 - SLOTS, 128), F32)], axis=0))
+        rest = jnp.zeros((32, 128), F32)
+        for c in range(4):
+            rest = rest + pltpu.roll(jnp.where(fifth, x[32 * c : 32 * c + 32], 0.0), 128 + c - 4, 1)
+        x = jnp.concatenate([x, rest], axis=0)
         left = jnp.where(column == 0, 0.0, pltpu.roll(x, 1, 0))
         right = jnp.where(column == W - 1, 0.0, pltpu.roll(x, W - 1, 0))
-        ltt[k, :, 0:128] = (left + pltpu.roll(x, 64, 1)).astype(BF16)
-        ltt[k, :, 128:256] = right.astype(BF16)
+        centre = pltpu.roll(x, SLOTS, 1)
+        ltt[k, :, 0:128] = jnp.where(lane < SLOTS, left, centre).astype(BF16)
+        ltt[k, :, 128:256] = jnp.where(lane < 2 * SLOTS - 128, centre, pltpu.roll(right, 2 * SLOTS - 128, 1)).astype(BF16)
 
     def send_time_stats(e, s, q):
         tstbuf[e, rr, 0:1] = jnp.sum(s, axis=0, keepdims=True)
@@ -483,7 +514,7 @@
             for n in (2 * m, 2 * m + 1):
                 at = R * rr + n - margin
                 ok = jnp.logical_and(jnp.logical_and(at >= 0, at < n_rows * R), f >= g)
-                a = jnp.where(ok, half_silu(src[g, n], scale, shift), 0.0)
+                a = half_silu(src[g, n], jnp.where(ok, scale, 0.0), jnp.where(ok, shift, 0.0))
                 for j, x in enumerate(column_shifts(a)):
                     dst[g, n, :, T * j : T * j + T] = x
             return 0
@@ -597,7 +628,7 @@
     dma = pltpu.SemaphoreType.DMA
     result = pl.pallas_call(
         functools.partial(kernel, n_frames, n_rows),
-        out_shape=jax.ShapeDtypeStruct((R, W, T), BF16),
+        out_shape=pltpu.VMEM((R, W, T), BF16),
         in_specs=[pl.BlockSpec(memory_space=pl.ANY)] * len(args),
         out_specs=pl.BlockSpec(memory_space=pltpu.VMEM),
         scratch_shapes=[
@@ -612,7 +643,7 @@
             vmem(2, W, C),
             vmem(2, W, C),
             vmem(6, 4, 128, dtype=F32),
-            vmem(2, 1, C, dtype=F32),
+            vmem(2, 2, 1, HALF, dtype=F32),
             vmem(6, 1, T, dtype=F32),
             vmem(1, 8, dtype=F32),
             vmem(4, 8, dtype=F32),
@@ -627,15 +658,15 @@
             vmem(3, 4, 3 * T, 2 * T),
             vmem(4, n_rows, 8, 128, dtype=F32),
             vmem(8, n_rows, 8, 128, dtype=F32),
-            vmem(4 * R, LANES),
-            vmem(BACK + 1, 64, LANES),
+            vmem(64, 128),
+            vmem(BACK + 1, SLOTS, 128),
             vmem(BACK + 1, W, 256),
             vmem(5, R + 4, W, T, dtype=F32),
             vmem(5, R + 4, W, 3 * T),
             vmem(3, R + 2, W, T, dtype=F32),
             vmem(3, R + 2, W, 3 * T),
             vmem(R // 2 * W, 2 * T, dtype=F32),
-            dma((28,)),
+            dma((29,)),
             dma((4,)),
             dma((2, 4)),
             dma((4,)),

time: 60.4 us -> 57.2 us (0.947)
  Pallas kernels: 58.5 us -> 56.4 us
  local copies, waits for them, and re-layouts: 1.72 us -> 0.73 us
    pallas_call x1, Pallas kernels: 58.5 us -> 56.4 us  [body(): pl.pallas_call(functools.partial(kernel, n_frames, n_rows), out_shape=plt...]
    unnamed x1, local copies, waits for them, and re-layouts: 1.72 us -> 0.73 us
where the time goes in v2:
time: 57.2 us
  Pallas kernels  56.4 us (99%)
  local copies, waits for them, and re-layouts  0.73 us (1%)
    pallas_call x1, Pallas kernels, body(): pl.pallas_call(functools.partial(kernel, n_frames, n_rows), out_shape=plt...  56.4 us

profile of v2, /device:TPU:17, one launch (start us, length us, event | category | flops | bytes accessed | tf_op | source)
XLA Modules:
  0.0 57.2 jit_solution(18007064988119671602)
XLA Ops:
  0.0 56.4 %encoder_window.1 = bf16[8,160,128]{2,1,0:T(8,128)(2,1)S(1)} custom-call(bf16[8,160,512]{2,1,0:T(8,128)(2,1)} %bitcast.29, f32[4,128]{1,0:T(4,128)} %bitcast.33, f32[4,128]{1,0:T(4,128)} %bitcast.34, bf16[9,512,512]{2,1,0:T(8,128)(2,1)} %bitcast.27, f32[1,512]{1,0:T(1,128)} %bitcast.35, f32[4,128]{1,0:T(4,128)} %bitcast.36, f32[4,128]{1,0:T(4,128)} %bitcast.37, ...), custom_call_target="tpu_custom_call" | custom-call | tf_op jit(solution)/shard_map/encoder_window/pallas_call | solution.py:629
  56.4 0.7 %copy.26 = bf16[1,8,160,128]{3,2,1,0:T(8,128)(2,1)} copy(bf16[1,8,160,128]{3,2,1,0:T(8,128)(2,1)S(1)} %bitcast.26) | data formatting | bytes 655360

commit v3 on v2

--- a/solution.py
+++ b/solution.py
@@ -72,8 +72,8 @@
     vid, w1, w2, act, h, yp, hsend, hrecv, ysend, yrecv,
     params, cbias, tparams, obv, qwv, qbv, tiwv,
     wht, pt, mom, wbf, wb, w1r, w2r,
-    stbuf, tstbuf, latsend, lx, ltt, t0s, b1, t1s, b2, facc,
-    in_sem, vh_sem, hh_sem, yh_sem, st_sem, lat_send, lat_recv,
+    stbuf, tstbuf, latsend, lx, ltt, t0s, b1, t1s, t1send, t1recv, b2, facc,
+    in_sem, vh_sem, hh_sem, yh_sem, th_sem, st_sem, lat_send, lat_recv,
 ):
     f = lax.axis_index("frames")
     rr = lax.axis_index("rows")
@@ -288,11 +288,10 @@
         for j in range(3):
             for i in range(3):
                 piece = tiwv[t, i, j].astype(F32)
-                for n in range(R + 4):
-                    top = SLOTS * j + packed_row(n + i - 3)
+                for n in range(R + 2):
+                    top = SLOTS * j + packed_row(n + i - 2)
                     wbf[top : top + 4, T * n : T * n + T] = piece
-        for n in range(3):
-            wb[n, 256 * t : 256 * t + 256] = wbf[:, 512 * n : 512 * n + 512].astype(BF16)
+        wb[256 * t : 256 * t + 256] = wbf[...].astype(BF16)
 
     finish(c_par + c_cb)
     scale, shift = norm_terms(0, copies, params[0], params[1])
@@ -507,19 +506,9 @@
         scale = lax.rsqrt(var + EPS) * gain
         return 0.5 * scale, 0.5 * (shift - mean * scale)
 
-    def time_lines(src, dst, g, n_lines, margin, terms):
-        scale, shift = terms
-
-        def lines(m, _):
-            for n in (2 * m, 2 * m + 1):
-                at = R * rr + n - margin
-                ok = jnp.logical_and(jnp.logical_and(at >= 0, at < n_rows * R), f >= g)
-                a = half_silu(src[g, n], jnp.where(ok, scale, 0.0), jnp.where(ok, shift, 0.0))
-                for j, x in enumerate(column_shifts(a)):
-                    dst[g, n, :, T * j : T * j + T] = x
-            return 0
-
-        lax.fori_loop(0, n_lines // 2, lines, 0)
+    def time_line(dst, g, n, v, scale, shift):
+        for j, x in enumerate(column_shifts(half_silu(v, scale, shift))):
+            dst[g, n, :, T * j : T * j + T] = x
 
     def pair_lines(src, g, i, pairs):
         return jnp.concatenate([src[g, 2 * p + i] for p in range(pairs)], axis=0)
@@ -532,15 +521,14 @@
         lhs = jnp.concatenate([ltt[g + 2], ltt[g + 1], ltt[g]], axis=1)
         s = jnp.zeros((8, T), F32)
         q = jnp.zeros((8, T), F32)
-        for n in range(3):
-            acc = jnp.dot(lhs, wb[n], preferred_element_type=F32)
-            for m in range(4):
-                v = acc[:, T * m : T * m + T] + tparams[0]
-                t0s[g, 4 * n + m] = v
-                if 2 <= 4 * n + m < R + 2:
-                    a, c = partial_sums(v)
-                    s += a
-                    q += c
+        acc = jnp.dot(lhs, wb[...], preferred_element_type=F32)
+        for n in range(R + 2):
+            v = acc[:, T * n : T * n + T] + tparams[0]
+            t0s[g, n] = v
+            if 1 <= n < R + 1:
+                a, c = partial_sums(v)
+                s += a
+                q += c
         send_time_stats(g, s, q)
         return 0
 
@@ -549,7 +537,16 @@
     finish(c_t)
 
     def b1_frame(g):
-        time_lines(t0s, b1, g, R + 4, 2, time_terms(g, tparams[1], tparams[2]))
+        scale, shift = time_terms(g, tparams[1], tparams[2])
+
+        def lines(m, _):
+            for n in (2 * m, 2 * m + 1):
+                at = R * rr + n - 1
+                ok = jnp.logical_and(jnp.logical_and(at >= 0, at < n_rows * R), f >= g)
+                time_line(b1, g, n, t0s[g, n], jnp.where(ok, scale, 0.0), jnp.where(ok, shift, 0.0))
+            return 0
+
+        lax.fori_loop(0, R // 2 + 1, lines, 0)
 
     def b1_first(g, _):
         b1_frame(g)
@@ -557,9 +554,15 @@
 
     lax.fori_loop(0, 2, b1_first, 0)
 
+    pairs = R // 2
+
+    def th(g):
+        return halo(
+            t1send.at[g, 1], t1send.at[g, 0], t1recv.at[g, 0], t1recv.at[g, 1], th_sem.at[g]
+        )
+
     def t1_frame(g, _):
         b1_frame(g + 2)
-        pairs = R // 2 + 1
         lhs = jnp.concatenate(
             [pair_lines(b1, g + 2 - t, i, pairs) for t in range(3) for i in range(4)], axis=1
         )
@@ -570,21 +573,43 @@
             for half in range(2):
                 v = acc[W * p : W * p + W, T * half : T * half + T]
                 t1s[g, 2 * p + half] = v
-                if 1 <= 2 * p + half < R + 1:
-                    a, c = partial_sums(v)
-                    s += a
-                    q += c
+                if 2 * p + half in (0, R - 1):
+                    t1send[g, half] = v.astype(BF16)
+                a, c = partial_sums(v)
+                s += a
+                q += c
         send_time_stats(5 + g, s, q)
+        start_down(th(g))
+        start_up(th(g))
         return 0
 
     lax.fori_loop(0, 3, t1_frame, 0)
 
     for p in range(R // 2):
         for half in range(2):
-            facc[W * p : W * p + W, T * half : T * half + T] = t0s[0, 2 * p + half + 2] + tparams[5]
+            facc[W * p : W * p + W, T * half : T * half + T] = t0s[0, 2 * p + half + 1] + tparams[5]
 
     def feature_frame(g, _):
-        time_lines(t1s, b2, g, R + 2, 1, time_terms(5 + g, tparams[3], tparams[4]))
+        scale, shift = time_terms(5 + g, tparams[3], tparams[4])
+        scale = jnp.where(f >= g, scale, 0.0)
+        shift = jnp.where(f >= g, shift, 0.0)
+
+        def lines(m, _):
+            for n in (2 * m, 2 * m + 1):
+                time_line(b2, g, n + 1, t1s[g, n], scale, shift)
+            return 0
+
+        lax.fori_loop(0, R // 2, lines, 0)
+        for has, copy, side, n in ((has_above, th(g)[0], 0, 0), (has_below, th(g)[1], 1, R + 1)):
+            @pl.when(has)
+            def _():
+                copy.wait_recv()
+                time_line(b2, g, n, t1recv[g, side].astype(F32), scale, shift)
+
+            @pl.when(jnp.logical_not(has))
+            def _():
+                b2[g, n] = jnp.zeros((W, 3 * T), BF16)
+
         lhs = jnp.concatenate([pair_lines(b2, g, i, R // 2) for i in range(4)], axis=1)
         facc[...] += jnp.dot(
             lhs, w2r[2 - g].reshape(4 * 3 * T, 2 * T), preferred_element_type=F32
@@ -600,6 +625,8 @@
     end_sends(hh[0])
     end_sends(hh[1])
     end_sends(yh)
+    for g in range(3):
+        end_sends(th(g))
     for k, d in lat_targets():
         @pl.when(sends_to(k, d))
         def _():
@@ -652,8 +679,8 @@
             vmem(72, C),
             vmem(R + 2, 72, LANES, dtype=F32),
             vmem(8 * R, LANES, dtype=F32),
-            vmem(256, 12 * T, dtype=F32),
-            vmem(3, 768, 4 * T),
+            vmem(256, (R + 2) * T, dtype=F32),
+            vmem(768, (R + 2) * T),
             vmem(3, 4, 3 * T, 2 * T),
             vmem(3, 4, 3 * T, 2 * T),
             vmem(4, n_rows, 8, 128, dtype=F32),
@@ -661,15 +688,18 @@
             vmem(64, 128),
             vmem(BACK + 1, SLOTS, 128),
             vmem(BACK + 1, W, 256),
-            vmem(5, R + 4, W, T, dtype=F32),
-            vmem(5, R + 4, W, 3 * T),
-            vmem(3, R + 2, W, T, dtype=F32),
+            vmem(5, R + 2, W, T, dtype=F32),
+            vmem(5, R + 2, W, 3 * T),
+            vmem(3, R, W, T, dtype=F32),
+            vmem(3, 2, W, T),
+            vmem(3, 2, W, T),
             vmem(3, R + 2, W, 3 * T),
             vmem(R // 2 * W, 2 * T, dtype=F32),
             dma((29,)),
             dma((4,)),
             dma((2, 4)),
             dma((4,)),
+            dma((3, 4)),
             dma((12, 2, n_rows - 1)),
             dma((BACK + 1, 3)),
             dma((BACK + 1, 3)),

time: 57.2 us -> 55.6 us (0.972)
  Pallas kernels: 56.4 us -> 54.7 us
    pallas_call x1, Pallas kernels: 56.4 us -> 54.7 us  [body(): pl.pallas_call(functools.partial(kernel, n_frames, n_rows), out_shape=plt...]
where the time goes in v3:
time: 55.6 us; the launch traced here: 55.5 us
  Pallas kernels  54.7 us (98%)
  local copies, waits for them, and re-layouts  0.73 us (1%)
    pallas_call x1, Pallas kernels, body(): pl.pallas_call(functools.partial(kernel, n_frames, n_rows), out_shape=plt...  54.7 us

profile of v3, /device:TPU:17, one launch (start us, length us, event | category | flops | bytes accessed | tf_op | source)
XLA Modules:
  0.0 55.5 jit_solution(139414454126779713)
XLA Ops:
  0.0 54.7 %encoder_window.1 = bf16[8,160,128]{2,1,0:T(8,128)(2,1)S(1)} custom-call(bf16[8,160,512]{2,1,0:T(8,128)(2,1)} %bitcast.29, f32[4,128]{1,0:T(4,128)} %bitcast.33, f32[4,128]{1,0:T(4,128)} %bitcast.34, bf16[9,512,512]{2,1,0:T(8,128)(2,1)} %bitcast.27, f32[1,512]{1,0:T(1,128)} %bitcast.35, f32[4,128]{1,0:T(4,128)} %bitcast.36, f32[4,128]{1,0:T(4,128)} %bitcast.37, ...), custom_call_target="tpu_custom_call" | custom-call | tf_op jit(solution)/shard_map/encoder_window/pallas_call | solution.py:656
  54.7 0.7 %copy.26 = bf16[1,8,160,128]{3,2,1,0:T(8,128)(2,1)} copy(bf16[1,8,160,128]{3,2,1,0:T(8,128)(2,1)S(1)} %bitcast.26) | data formatting | bytes 655360

commit v4 on v3

--- a/solution.py
+++ b/solution.py
@@ -83,7 +83,7 @@
 
     c_vid = local(video, vid.at[pl.ds(1, R)], 0)
     c_w1 = [local(cw1.at[:, :, pl.ds(HALF * i, HALF)], w1.at[i], (1, 26)[i]) for i in range(2)]
-    c_w2 = local(cw2, w2, 2)
+    c_w2 = [local(cw2.at[:, :, pl.ds(HALF * i, HALF)], w2.at[i], (2, 29)[i]) for i in range(2)]
     c_par = [local(a, params.at[i], 3 + i) for i, a in enumerate((g1, s1, g2, s2, g3, s3))]
     c_cb = [
         local(a.at[:, pl.ds(HALF * n, HALF)], cbias.at[i, n], (9, 27)[n] + i)
@@ -279,7 +279,7 @@
     vh = halo(vid.at[R], vid.at[1], vid.at[0], vid.at[R + 1], vh_sem)
     start_down(vh)
     start_up(vh)
-    c_w2.start()
+    begin(c_w2)
     begin(c_t)
 
     finish([c_tiw])
@@ -342,9 +342,9 @@
         halo_lines(hh[half], hrecv.at[half, 0], hrecv.at[half, 1], scale, shift, (half,))
 
     h_norm(0)
-    c_w2.wait()
-
-    yh = halo(ysend.at[1], ysend.at[0], yrecv.at[0], yrecv.at[1], yh_sem)
+    finish(c_w2)
+
+    yh = [halo(ysend.at[i, 1], ysend.at[i, 0], yrecv.at[i, 0], yrecv.at[i, 1], yh_sem.at[i]) for i in range(2)]
 
     def y_part(b, lo, hi, acc, s, q):
         res = jnp.concatenate(
@@ -352,37 +352,37 @@
             axis=0,
         )
         v = res.astype(F32) + (acc + jnp.concatenate([cbias[1, 0], cbias[1, 1]], axis=1))
-        yp[pl.ds(lo, 2)] = v[: 2 * W].reshape(2, W, C)
-        yp[pl.ds(hi, 2)] = v[2 * W :].reshape(2, W, C)
-        return s, q
-
-    def y_lines(b, lo, hi, acc, s, q):
-        part = jnp.concatenate(
-            [yp[pl.ds(lo, 2)].reshape(2 * W, C), yp[pl.ds(hi, 2)].reshape(2 * W, C)], axis=0
-        )
-        v = part + acc
         for half in range(2):
             x = v[:, HALF * half : HALF * half + HALF]
-            h[half, pl.ds(lo, 2)] = x[: 2 * W].reshape(2, W, HALF)
-            h[half, pl.ds(hi, 2)] = x[2 * W :].reshape(2, W, HALF)
-
-        @pl.when(b == 0)
-        def _():
-            ysend[0] = v[:W].astype(BF16)
-            ysend[1] = v[3 * W :].astype(BF16)
-            start_down(yh)
-            start_up(yh)
-
-        a, c = partial_sums(v)
-        return s + a, q + c
-
-    conv(lambda j, line: two_lines(0, j, line), lambda tap: w2[tap, 0:HALF], C, y_part)
+            yp[half, pl.ds(lo, 2)] = x[: 2 * W].reshape(2, W, HALF)
+            yp[half, pl.ds(hi, 2)] = x[2 * W :].reshape(2, W, HALF)
+        return s, q
+
+    conv(lambda j, line: two_lines(0, j, line), lambda tap: jnp.concatenate([w2[0, tap, 0:HALF], w2[1, tap, 0:HALF]], axis=1), C, y_part)
 
     h_norm(1)
 
-    s, q = conv(lambda j, line: two_lines(1, j, line), lambda tap: w2[tap, HALF:C], C, y_lines)
-
-    copies = send_stats(3, s, q)
+    def y_half(half, _):
+        acc = None
+        for i in range(3):
+            for j in range(3):
+                lhs = act[1, j, i : i + R].reshape(R * W, HALF)
+                d = jnp.dot(lhs, w2[half, 3 * i + j, HALF:C], preferred_element_type=F32)
+                acc = d if acc is None else acc + d
+        v = yp[half].reshape(R * W, HALF) + acc
+        h[half] = v.reshape(R, W, HALF)
+        ysend[half, 0] = v[:W].astype(BF16)
+        ysend[half, 1] = v[R * W - W :].astype(BF16)
+        copies = halo(
+            ysend.at[half, 1], ysend.at[half, 0], yrecv.at[half, 0], yrecv.at[half, 1], yh_sem.at[half]
+        )
+        send_stats(3 + half, *partial_sums(v))
+        start_down(copies)
+        start_up(copies)
+        return 0
+
+    lax.fori_loop(0, 2, y_half, 0)
+
     finish([c_ow] + c_q + c_tp)
     nt = (((1,), (1,)), ((), ()))
     pt[...] = jnp.zeros(pt.shape, F32)
@@ -406,19 +406,25 @@
     for c in range(4):
         quant_bias = quant_bias + jnp.where(row5 % 5 == c, qbv[0:1, c : c + 1], 0.0)
 
-    scale, shift = norm_terms(3, copies, params[4], params[5])
-
-    def y_line(r, _):
-        v = jnp.concatenate([h[0, r], h[1, r]], axis=1)
-        put_line(r + 1, v, scale, shift, shifted=False)
-        return 0
-
-    lax.fori_loop(0, R, y_line, 0)
-    halo_lines(yh, yrecv.at[0], yrecv.at[1], scale, shift, shifted=False)
-
+    def y_norm(half):
+        scale, shift = norm_terms(
+            3 + half, stat_copies(stbuf.at[3 + half], 3 + half),
+            params[4, 2 * half : 2 * half + 2], params[5, 2 * half : 2 * half + 2],
+        )
+
+        def y_line(r, _):
+            put_line(r + 1, h[half, r], scale, shift, (half,), shifted=False)
+            return 0
+
+        lax.fori_loop(0, R, y_line, 0)
+        halo_lines(yh[half], yrecv.at[half, 0], yrecv.at[half, 1], scale, shift, (half,), shifted=False)
+
+    y_norm(0)
     for r in range(R + 2):
-        line = jnp.concatenate([act[0, 1, r], act[1, 1, r]], axis=1)
-        pt[r, :, 0:W] = lax.dot_general(wht[...], line, nt, preferred_element_type=F32)
+        pt[r, :, 0:W] = lax.dot_general(wht[:, 0:HALF], act[0, 1, r], nt, preferred_element_type=F32)
+    y_norm(1)
+    for r in range(R + 2):
+        pt[r, :, 0:W] += lax.dot_general(wht[:, HALF:C], act[1, 1, r], nt, preferred_element_type=F32)
     for r in range(R):
         sums = []
         for j in range(3):
@@ -493,10 +499,10 @@
     def send_time_stats(e, s, q):
         tstbuf[e, rr, 0:1] = jnp.sum(s, axis=0, keepdims=True)
         tstbuf[e, rr, 1:2] = jnp.sum(q, axis=0, keepdims=True)
-        begin(stat_copies(tstbuf.at[e], 4 + e))
+        begin(stat_copies(tstbuf.at[e], 5 + e))
 
     def time_terms(e, gain, shift):
-        finish(stat_copies(tstbuf.at[e], 4 + e))
+        finish(stat_copies(tstbuf.at[e], 5 + e))
         total = tstbuf[e, 0]
         for r in range(1, n_rows):
             total = total + tstbuf[e, r]
@@ -624,7 +630,8 @@
     end_sends(vh)
     end_sends(hh[0])
     end_sends(hh[1])
-    end_sends(yh)
+    end_sends(yh[0])
+    end_sends(yh[1])
     for g in range(3):
         end_sends(th(g))
     for k, d in lat_targets():
@@ -661,14 +668,14 @@
         scratch_shapes=[
             vmem(R + 2, W, C),
             vmem(2, 9, C, HALF),
-            vmem(9, C, C),
+            vmem(2, 9, C, HALF),
             vmem(2, 3, R + 2, W, HALF),
             vmem(2, R, W, HALF, dtype=F32),
-            vmem(R, W, C, dtype=F32),
+            vmem(2, R, W, HALF, dtype=F32),
             vmem(2, 2, W, HALF),
             vmem(2, 2, W, HALF),
-            vmem(2, W, C),
-            vmem(2, W, C),
+            vmem(2, 2, W, HALF),
+            vmem(2, 2, W, HALF),
             vmem(6, 4, 128, dtype=F32),
             vmem(2, 2, 1, HALF, dtype=F32),
             vmem(6, 1, T, dtype=F32),
@@ -683,7 +690,7 @@
             vmem(768, (R + 2) * T),
             vmem(3, 4, 3 * T, 2 * T),
             vmem(3, 4, 3 * T, 2 * T),
-            vmem(4, n_rows, 8, 128, dtype=F32),
+            vmem(5, n_rows, 8, 128, dtype=F32),
             vmem(8, n_rows, 8, 128, dtype=F32),
             vmem(64, 128),
             vmem(BACK + 1, SLOTS, 128),
@@ -695,12 +702,12 @@
             vmem(3, 2, W, T),
             vmem(3, R + 2, W, 3 * T),
             vmem(R // 2 * W, 2 * T, dtype=F32),
-            dma((29,)),
+            dma((30,)),
             dma((4,)),
             dma((2, 4)),
-            dma((4,)),
+            dma((2, 4)),
             dma((3, 4)),
-            dma((12, 2, n_rows - 1)),
+            dma((13, 2, n_rows - 1)),
             dma((BACK + 1, 3)),
             dma((BACK + 1, 3)),
         ],

time: 55.6 us -> 54.7 us (0.984)
  Pallas kernels: 54.7 us -> 53.9 us
    pallas_call x1, Pallas kernels: 54.7 us -> 53.9 us  [body(): pl.pallas_call(functools.partial(kernel, n_frames, n_rows), out_shape=plt...]
where the time goes in v4:
time: 54.7 us; the launch traced here: 54.6 us
  Pallas kernels  53.9 us (99%)
  local copies, waits for them, and re-layouts  0.73 us (1%)
    pallas_call x1, Pallas kernels, body(): pl.pallas_call(functools.partial(kernel, n_frames, n_rows), out_shape=plt...  53.9 us

profile of v4, /device:TPU:17, one launch (start us, length us, event | category | flops | bytes accessed | tf_op | source)
XLA Modules:
  0.0 54.6 jit_solution(2188714821098067988)
XLA Ops:
  0.0 53.9 %encoder_window.1 = bf16[8,160,128]{2,1,0:T(8,128)(2,1)S(1)} custom-call(bf16[8,160,512]{2,1,0:T(8,128)(2,1)} %bitcast.29, f32[4,128]{1,0:T(4,128)} %bitcast.33, f32[4,128]{1,0:T(4,128)} %bitcast.34, bf16[9,512,512]{2,1,0:T(8,128)(2,1)} %bitcast.27, f32[1,512]{1,0:T(1,128)} %bitcast.35, f32[4,128]{1,0:T(4,128)} %bitcast.36, f32[4,128]{1,0:T(4,128)} %bitcast.37, ...), custom_call_target="tpu_custom_call" | custom-call | tf_op jit(solution)/shard_map/encoder_window/pallas_call | solution.py:663
  53.9 0.7 %copy.26 = bf16[1,8,160,128]{3,2,1,0:T(8,128)(2,1)} copy(bf16[1,8,160,128]{3,2,1,0:T(8,128)(2,1)S(1)} %bitcast.26) | data formatting | bytes 655360

commit v5 on v4

--- a/solution.py
+++ b/solution.py
@@ -546,13 +546,13 @@
         scale, shift = time_terms(g, tparams[1], tparams[2])
 
         def lines(m, _):
-            for n in (2 * m, 2 * m + 1):
+            for n in [5 * m + i for i in range(5)]:
                 at = R * rr + n - 1
                 ok = jnp.logical_and(jnp.logical_and(at >= 0, at < n_rows * R), f >= g)
                 time_line(b1, g, n, t0s[g, n], jnp.where(ok, scale, 0.0), jnp.where(ok, shift, 0.0))
             return 0
 
-        lax.fori_loop(0, R // 2 + 1, lines, 0)
+        lax.fori_loop(0, (R + 2) // 5, lines, 0)
 
     def b1_first(g, _):
         b1_frame(g)
@@ -601,11 +601,11 @@
         shift = jnp.where(f >= g, shift, 0.0)
 
         def lines(m, _):
-            for n in (2 * m, 2 * m + 1):
+            for n in [4 * m + i for i in range(4)]:
                 time_line(b2, g, n + 1, t1s[g, n], scale, shift)
             return 0
 
-        lax.fori_loop(0, R // 2, lines, 0)
+        lax.fori_loop(0, R // 4, lines, 0)
         for has, copy, side, n in ((has_above, th(g)[0], 0, 0), (has_below, th(g)[1], 1, R + 1)):
             @pl.when(has)
             def _():

time: 54.7 us -> 54.5 us (level)
  no operation moved by 1% of the time
where the time goes in v5:
time: 54.5 us; the launch traced here: 54.4 us
  Pallas kernels  53.6 us (98%)
  local copies, waits for them, and re-layouts  0.73 us (1%)
    pallas_call x1, Pallas kernels, body(): pl.pallas_call(functools.partial(kernel, n_frames, n_rows), out_shape=plt...  53.6 us

profile of v5, /device:TPU:17, one launch (start us, length us, event | category | flops | bytes accessed | tf_op | source)
XLA Modules:
  0.0 54.4 jit_solution(8720135774604926542)
XLA Ops:
  0.0 53.6 %encoder_window.1 = bf16[8,160,128]{2,1,0:T(8,128)(2,1)S(1)} custom-call(bf16[8,160,512]{2,1,0:T(8,128)(2,1)} %bitcast.29, f32[4,128]{1,0:T(4,128)} %bitcast.33, f32[4,128]{1,0:T(4,128)} %bitcast.34, bf16[9,512,512]{2,1,0:T(8,128)(2,1)} %bitcast.27, f32[1,512]{1,0:T(1,128)} %bitcast.35, f32[4,128]{1,0:T(4,128)} %bitcast.36, f32[4,128]{1,0:T(4,128)} %bitcast.37, ...), custom_call_target="tpu_custom_call" | custom-call | tf_op jit(solution)/shard_map/encoder_window/pallas_call | solution.py:663
  53.7 0.7 %copy.26 = bf16[1,8,160,128]{3,2,1,0:T(8,128)(2,1)} copy(bf16[1,8,160,128]{3,2,1,0:T(8,128)(2,1)S(1)} %bitcast.26) | data formatting | bytes 655360
